TPU v7x, 32 devices: a whole 2x2x4 slice. The times are simulated.
32 devices in a mesh: dp: 8 (over y, x, core), seq: 4 (over z).
Axes of the slice: x: 2, y: 2, z: 4, core: 2. Of those that a mesh axis runs over, the one named last changes fastest.
Arguments:
- tile_tokens: bfloat16 [8, 128, 3200], P('dp', 'seq'), may hold values from -6 to 6
- proj_weight: bfloat16 [3200, 8192], P('dp', 'seq')
- text_hidden: bfloat16 [8, 512, 8192], P('dp', 'seq'), may hold values from -6 to 6
- cotangent: bfloat16 [8, 512, 8192], P('dp', 'seq'), may hold values from -1.1953125 to 1.1953125
- norm_gain: float32 [8192], replicated, may hold values from 0.25 to 1.75
- placeholders: int32 [8, 128], P('dp'), may hold values from 0 to 511, as said below
- bucket_levels: int32 [8, 4, 3200], P('dp', 'seq'), may hold values from 2 to 16
- row_draws: float32 [8, 4, 3200], P('dp', 'seq'), may hold values from 0 to 1
- column_draws: float32 [8, 8192], P('dp', 'seq'), may hold values from 0 to 1
Outputs:
- weight_grad: float32 [3200, 8192], P('dp', 'seq')
- gain_grad: float32 [8192], replicated
Inputs may be any that keep to these rules, and one draw needn't show every extreme that they name: Each row is strictly increasing. Among the positions of one device's block of 128 positions stand at most 48 placeholders, and in every row some block holds exactly 48.
All inputs are finite; a program needn't handle non-finite values.
Results may differ from a plain program's by a relative error of at most 0.014.
Values may be sent and summed in bfloat16 or wider, within the bound.
No kernel may reach another device: no remote copies, remote signals or barrier semaphores. Data moves between devices by JAX's collectives and lax.ppermute only.
A program may use at most 64 MiB of HBM per device.

v0:
```python
import jax
import jax.numpy as jnp
from jax import lax
from jax.sharding import PartitionSpec as P

IMG_MOST = 48
EPSILON = 1e-06


def quantize(gradient, levels_now, rows_now, columns_now):
    bucket_norm = jnp.sqrt(jnp.sum(gradient * gradient, axis=1, keepdims=True) + EPSILON)
    step_count = levels_now.astype(jnp.float32)[:, None]
    offset = 0.25 + 0.25 * (rows_now[:, None] + columns_now[None, :])
    ratio = jnp.abs(gradient) / bucket_norm * step_count
    lower = jnp.floor(ratio)
    quantum = lower + jnp.clip(2.0 * (ratio - lower - offset) + 0.5, 0.0, 1.0)
    return jnp.sign(gradient) * bucket_norm * quantum / step_count


def on_device(
    tile_tokens,
    proj_weight,
    text_hidden,
    cotangent,
    norm_gain,
    placeholders,
    bucket_levels,
    row_draws,
    column_draws,
):
    seq_count = lax.axis_size("seq")
    seq_index = lax.axis_index("seq")
    replicas = lax.axis_size("dp")
    places = placeholders[0]
    image_total = places.shape[0]
    tok_rows = text_hidden.shape[1]
    model_width = text_hidden.shape[2]
    columns = proj_weight.shape[1]
    all_positions = tok_rows * seq_count
    zero_half = jnp.zeros((), jnp.bfloat16)
    own_text = text_hidden[0]
    own_cot = cotangent[0]
    gathered = lax.all_gather(tile_tokens[0], "seq", axis=0, tiled=True)
    patch_block = gathered
    embedded = jnp.dot(
        patch_block,
        lax.all_gather(proj_weight, "dp", axis=0, tiled=True),
        preferred_element_type=jnp.float32,
    ).astype(jnp.bfloat16)
    image_marks = jnp.zeros((all_positions,), jnp.int32).at[places].set(1)
    local_marks = lax.dynamic_slice_in_dim(image_marks, seq_index * tok_rows, tok_rows)
    is_image = local_marks[:, None] == 1
    owners = places // tok_rows
    owner_ids = jnp.arange(seq_count, dtype=jnp.int32)
    counts = jnp.sum((owners[:, None] == owner_ids[None, :]).astype(jnp.int32), axis=0)
    starts = jnp.cumsum(counts) - counts
    own_start = starts[seq_index]
    own_count = counts[seq_index]
    slot_ids = jnp.arange(IMG_MOST, dtype=jnp.int32)
    source_rows = jnp.clip(own_start + slot_ids, 0, image_total - 1)
    local_slots = jnp.clip(jnp.take(places, source_rows) - seq_index * tok_rows, 0, tok_rows - 1)
    slot_live = (slot_ids < own_count)[:, None]
    flat_index = owners * IMG_MOST + (
        jnp.arange(image_total, dtype=jnp.int32) - jnp.take(starts, owners)
    )
    outgoing = jnp.where(slot_live, jnp.take(own_cot, local_slots, axis=0), zero_half)
    returned = lax.all_to_all(outgoing[None], "seq", split_axis=2, concat_axis=0, tiled=True)
    image_cot = jnp.take(returned.reshape(-1, columns), flat_index, axis=0).astype(jnp.float32)
    emb_float = embedded.astype(jnp.float32)
    column_gain = lax.dynamic_slice_in_dim(norm_gain, seq_index * columns, columns)
    grad_in = image_cot * column_gain[None, :]
    squares, mixed = lax.psum(
        (jnp.sum(emb_float * emb_float, axis=1), jnp.sum(grad_in * emb_float, axis=1)), "seq"
    )
    inverse = lax.rsqrt(squares / model_width + EPSILON)[:, None]
    normed = emb_float * inverse
    emb_grad = ((grad_in - normed * (mixed[:, None] * inverse / model_width)) * inverse).astype(
        jnp.bfloat16
    )
    image_part = jnp.sum(image_cot * normed, axis=0)
    text_float = own_text.astype(jnp.float32)
    text_inverse = lax.rsqrt(jnp.mean(text_float * text_float, axis=1, keepdims=True) + EPSILON)
    text_terms = own_cot.astype(jnp.float32) * text_float * text_inverse
    text_part = jnp.sum(jnp.where(is_image, 0.0, text_terms), axis=0)
    placed_part = lax.dynamic_update_slice_in_dim(
        jnp.zeros((model_width,), jnp.float32), image_part, seq_index * columns, 0
    )
    gain_part = text_part + placed_part
    own_levels = bucket_levels[0, 0]
    own_row_draws = row_draws[0, 0]
    own_column_draws = column_draws[0]
    patch_block = gathered
    gradient = lax.dot_general(
        patch_block, emb_grad, (((0,), (0,)), ((), ())), preferred_element_type=jnp.float32
    )
    summed = lax.psum_scatter(
        quantize(gradient, own_levels, own_row_draws, own_column_draws).astype(jnp.bfloat16),
        "dp",
        scatter_dimension=0,
        tiled=True,
    ).astype(jnp.float32)
    gain_total = lax.psum(gain_part, ("dp", "seq"))
    return (summed / replicas, gain_total / replicas)


def solution(mesh):
    return jax.shard_map(
        on_device,
        mesh=mesh,
        in_specs=(
            P("dp", "seq", None),
            P("dp", "seq"),
            P("dp", "seq", None),
            P("dp", "seq", None),
            P(),
            P("dp", None),
            P("dp", "seq", None),
            P("dp", "seq", None),
            P("dp", "seq"),
        ),
        out_specs=(P("dp", "seq"), P()),
        check_vma=False,
    )
```

profile of v0, /device:TPU:0, one launch (start us, length us, event | category | flops | bytes accessed | tf_op | source)
XLA Modules:
  0.0 315.0 jit_solution(2458585537406789046)
XLA Ops:
  7.2 0.0 copy-start
  7.2 0.0 all-gather.3.cloned.1.call-start
  7.3 0.7 all-gather.3.cloned.1.call-update
  7.9 0.7 and_select_fusion.5
  8.6 0.1 convert_reduce_fusion.1
  8.7 0.2 reduce-window.9
  8.9 0.6 dynamic_slice.12
  9.5 0.7 fusion.34
  10.2 0.7 fusion.33
  10.9 1.4 gather_fusion
  12.3 0.7 fusion.31
  13.0 3.6 %gather_fusion.1 = bf16[48,8192]{1,0:T(8,128)(2,1)S(1)} fusion(bf16[128,8192]{1,0:T(8,128)(2,1)} %bitcast.74, s32[1024]{0:T(1024)S(1)} %pad_clamp_fusion.1), kind=kCustom, calls=%fused_computation.1 | custom fusion | bytes 1573056 | tf_op jit(solution)/shard_map/jit(_take)/gather | solution.py:66
  16.6 1.3 compare_and_fusion
  17.9 0.2 fusion.21
  18.1 6.8 %copy.22 = bf16[1,48,8192]{1,0,2:T(2,128)(2,1)} copy(bf16[1,48,8192]{2,1,0:T(8,128)(2,1)S(1)} %fusion.21) | data formatting | bytes 1572864 | tf_op jit(solution)/shard_map/jit(_where)/select_n | solution.py:66
  24.8 0.5 broadcast.575
  25.3 45.2 %reduce.4 = bf16[8192,48]{1,0:T(8,128)(2,1)S(1)} reduce(bf16[8192,1,48]{2,1,0:T(2,128)(2,1)} %bitcast.76, bf16[]{:T(256)} %broadcast.575), dimensions={1}, to_apply=%bitcast.63.reduce_sub_computation | reduce | bytes 1572866
  70.6 4.0 %reshape.423 = bf16[4,2,49152]{2,1,0:T(2,128)(2,1)} reshape(bf16[8192,48]{1,0:T(8,128)(2,1)S(1)} %reduce.4) | data formatting | bytes 1572864
  74.6 6.3 %all-to-all-start = ((bf16[4,2,49152]{2,1,0:T(2,128)(2,1)}), bf16[4,2,49152]{2,1,0:T(2,128)(2,1)S(1)}, u32[]{:S(2)}, u32[]{:S(2)}) async-start(bf16[4,2,49152]{2,1,0:T(2,128)(2,1)} %reshape.423), calls=%async_computation | async-start | bytes 1572864 | tf_op jit(solution)/shard_map/all_to_all | solution.py:67
  80.9 0.7 dynamic_slice.14
  81.7 2.6 compare_and_fusion.1
  84.4 30.7 %all-gather = bf16[1,128,3200]{2,1,0:T(8,128)(2,1)S(1)} all-gather(bf16[1,32,3200]{2,1,0:T(8,128)(2,1)S(1)} %copy-done.4), channel_id=2, replica_groups=mesh['dp'=8,'seq'=4] {'seq'}, dimensions={1}, use_global_device_ids=true | all-gather | bytes 1024000 | tf_op jit(solution)/shard_map/all_gather | solution.py:43
  115.0 4.6 %reshape.424 = bf16[8192,1,48]{2,1,0:T(2,128)(2,1)} reshape(bf16[4,2,49152]{2,1,0:T(2,128)(2,1)S(1)} %all-to-all-done) | data formatting | bytes 1572864
  119.6 8.1 %copy.23 = bf16[1,48,8192]{2,1,0:T(8,128)(2,1)S(1)} copy(bf16[1,48,8192]{1,0,2:T(2,128)(2,1)} %bitcast.77) | data formatting | bytes 1572864 | tf_op jit(solution)/shard_map/all_to_all | solution.py:67
  127.8 0.6 all_to_all.12
  128.4 0.4 copy.24
  128.8 0.9 gather_fusion.2
  129.8 0.0 all-gather.3.cloned.1.call-done
  129.8 7.1 %multiply_reduce_fusion.1 = (f32[128]{0:T(128)S(1)}, f32[128,2048]{1,0:T(8,128)S(1)}) fusion(bf16[3200,2048]{1,0:T(8,128)(2,1)} %all-gather.3.cloned.1.call-done, bf16[1,128,3200]{2,1,0:T(8,128)(2,1)S(1)} %all-gather), kind=kOutput, calls=%fused_computation.31 | convolution fusion | flops 1678770048 | bytes 14975488 | tf_op jit(solution)/shard_map/dot_general | solution.py:45
  136.8 0.0 copy-start.2
  136.9 11.1 %psum.21 = f32[128]{0:T(128)S(1)} all-reduce(f32[128]{0:T(128)S(1)} %get-tuple-element.22), channel_id=1, replica_groups=mesh['dp'=8,'seq'=4] {'seq'}, use_global_device_ids=true, to_apply=%region_3.4 | all-reduce | flops 128 | bytes 1024 | tf_op jit(solution)/shard_map/psum | solution.py:72
  148.0 0.4 fusion.17
  148.4 8.4 %psum.22 = f32[128]{0:T(128)S(1)} all-reduce(f32[128]{0:T(128)S(1)} %get-tuple-element.13), channel_id=1, replica_groups=mesh['dp'=8,'seq'=4] {'seq'}, use_global_device_ids=true, to_apply=%region_5.6 | all-reduce | flops 128 | bytes 1024 | tf_op jit(solution)/shard_map/psum | solution.py:72
  156.8 0.0 copy-start.7
  156.8 5.1 %multiply_reduce_fusion = (f32[3200]{0:T(1024)S(1)}, f32[2048,3200]{1,0:T(8,128)S(1)}) fusion(bf16[1,128,3200]{2,1,0:T(8,128)(2,1)S(1)} %all-gather, f32[128,2048]{1,0:T(8,128)} %copy-done.2, f32[128]{0:T(128)S(1)} %multiply_multiply_fusion, f32[128]{0:T(128)S(1)} %add_rsqrt_fusion.1, f32[2048]{0:T(1024)S(1)} %dynamic_slice.14, ...), kind=kOutput, calls=%fused_computation.12 | convolution fusion | flops 1692922752 | bytes 28628608 | tf_op jit(solution)/shard_map/dot_general | solution.py:93
  162.0 22.2 %fusion.6 = bf16[3200,2048]{0,1:T(8,128)(2,1)} fusion(f32[2048,3200]{1,0:T(8,128)S(1)} %get-tuple-element.25, f32[3200]{0:T(1024)S(1)} %convert_reduce_fusion, f32[2048]{0:T(1024)S(1)} %bitcast.79, f32[3200]{0:T(1024)S(1)} %reduce.2, f32[3200]{0:T(1024)S(1)} %add_sqrt_fusion), kind=kLoop, calls=%fused_computation.13 | loop fusion | flops 117964800 | bytes 39368192 | tf_op jit(solution)/shard_map/convert_element_type | solution.py:97
  184.1 18.3 %copy.26 = bf16[3200,2048]{1,0:T(8,128)(2,1)} copy(bf16[3200,2048]{0,1:T(8,128)(2,1)} %fusion.6) | data formatting | bytes 26214400
  202.5 0.0 reduce-scatter.4.cloned.1.call-update
  202.5 1.0 scatter_custom_fusion
  203.5 0.1 dynamic-slice_compare_fusion
  203.6 2.1 fusion.10
  205.7 2.6 fusion.9
  208.3 41.3 %psum.23 = f32[8192]{0:T(1024)S(1)} all-reduce(f32[8192]{0:T(1024)S(1)} %add_dynamic-update-slice_fusion), channel_id=1, replica_groups=mesh['dp'=8,'seq'=4] {'dp','seq'}, use_global_device_ids=true, to_apply=%region_12.13 | all-reduce | flops 8192 | bytes 65536 | tf_op jit(solution)/shard_map/psum | solution.py:102
  249.7 0.6 broadcast_multiply_fusion
  250.3 47.4 %reduce-scatter.4.cloned.1.call-done = bf16[400,2048]{1,0:T(8,128)(2,1)} async-done(((bf16[3200,2048]{1,0:T(8,128)(2,1)}), bf16[400,2048]{1,0:T(8,128)(2,1)}) %reduce-scatter.4.cloned.1.call-update) | async-done | bytes 1638416
  297.7 2.8 copy.27
  300.5 2.5 convert_multiply_fusion.2
  303.0 5.2 %copy.25 = f32[400,2048]{1,0:T(8,128)} copy(f32[400,2048]{0,1:T(8,128)} %convert_multiply_fusion.2) | data formatting | bytes 6553600
  (29 shorter events, 0.2 us)
Async XLA Ops:
  7.2 74.5 %copy-start = (s32[1,128]{1,0:T(1,128)S(1)}, s32[1,128]{1,0:T(1,128)}, u32[]{:S(2)}) copy-start(s32[1,128]{1,0:T(1,128)} %param.14) | copy-start | bytes 1540
  7.2 74.5 %copy-start.6 = (f32[1,1,3200]{2,1,0:T(1,128)S(1)}, f32[1,1,3200]{2,1,0:T(1,128)}, u32[]{:S(2)}) copy-start(f32[1,1,3200]{2,1,0:T(1,128)} %param.16) | copy-start | bytes 38404
  7.2 77.1 %copy-start.5 = (s32[1,1,3200]{2,1,0:T(1,128)S(1)}, s32[1,1,3200]{2,1,0:T(1,128)}, u32[]{:S(2)}) copy-start(s32[1,1,3200]{2,1,0:T(1,128)} %param.15) | copy-start | bytes 38404
  7.2 77.2 %copy-start.4 = (bf16[1,32,3200]{2,1,0:T(8,128)(2,1)S(1)}, bf16[1,32,3200]{2,1,0:T(8,128)(2,1)}, u32[]{:S(2)}) copy-start(bf16[1,32,3200]{2,1,0:T(8,128)(2,1)} %param.9) | copy-start | bytes 614404
  7.2 122.6 %all-gather.3.cloned.1.call-start = ((), (), s32[]{:S(2)}) async-start(), calls=%async_computation.2 | async-start | bytes 14745600 | tf_op jit(solution)/shard_map/all_gather | solution.py:47
  74.6 40.5 %all-to-all-start = ((bf16[4,2,49152]{2,1,0:T(2,128)(2,1)}), bf16[4,2,49152]{2,1,0:T(2,128)(2,1)S(1)}, u32[]{:S(2)}, u32[]{:S(2)}) async-start(bf16[4,2,49152]{2,1,0:T(2,128)(2,1)} %reshape.423), calls=%async_computation | async-start | bytes 1572864 | tf_op jit(solution)/shard_map/all_to_all | solution.py:67
  80.9 216.8 %reduce-scatter.4.cloned.1.call-start = ((), (), s32[]{:S(2)}) async-start(), calls=%async_computation.3 | async-start | bytes 14745600
  129.7 27.0 %copy-start.3 = (bf16[128,2048]{1,0:T(8,128)(2,1)}, bf16[128,2048]{1,0:T(8,128)(2,1)S(1)}, u32[]{:S(2)}) copy-start(bf16[128,2048]{1,0:T(8,128)(2,1)S(1)} %gather_fusion.2) | copy-start | bytes 1572868
  136.8 19.9 %copy-start.2 = (f32[128,2048]{1,0:T(8,128)}, f32[128,2048]{1,0:T(8,128)S(1)}, u32[]{:S(2)}) copy-start(f32[128,2048]{1,0:T(8,128)S(1)} %get-tuple-element.23) | copy-start | bytes 3145732
  156.8 5.2 %copy-start.7 = (f32[1,2048]{1,0:T(1,128)S(1)}, f32[1,2048]{1,0:T(1,128)}, u32[]{:S(2)}) copy-start(f32[1,2048]{1,0:T(1,128)} %param.17) | copy-start | bytes 24580
  202.5 3.2 %copy-start.1 = (bf16[1,128,8192]{2,1,0:T(8,128)(2,1)S(1)}, bf16[1,128,8192]{2,1,0:T(8,128)(2,1)}, u32[]{:S(2)}) copy-start(bf16[1,128,8192]{2,1,0:T(8,128)(2,1)} %param.12) | copy-start | bytes 6291460
Sparse Core Ops, SparseCore 0:
  9.9 76.9 all-gather.2
  202.6 95.0 reduce-scatter.3
where the time goes:
time: 316 us; the launch traced here: 315 us
  blocking collectives  91.5 us (29%)
  other arithmetic  82.2 us (26%)
  local copies, waits for them, and re-layouts  60.3 us (19%)
  waiting for transfers between devices  48.1 us (15%)
  between operations  14.3 us (5%)
  matrix products  12.2 us (4%)
  starting transfers between devices  6.39 us (2%)
    unnamed x3, waiting for transfers between devices  48.1 us
    unnamed x2, other arithmetic  45.3 us
    psum x1, blocking collectives, on_device(): gain_total = lax.psum(gain_part, ('dp', 'seq'))  41.3 us
    unnamed x22, local copies, waits for them, and re-layouts  35.4 us
    all_gather x1, blocking collectives, on_device(): gathered = lax.all_gather(tile_tokens[0], 'seq', axis=0, tiled=True)  30.7 us
    convert_element_type x1, other arithmetic, on_device(): quantize(gradient, own_levels, own_row_draws, own_column_draws)  22.2 us
    psum x2, blocking collectives, on_device(): lax.psum((jnp.sum(emb_float * emb_float, axis=1), jnp.sum(grad_in * emb_f...  19.5 us
    all_to_all x3, local copies, waits for them, and re-layouts, on_device(): lax.all_to_all(outgoing[None], 'seq', split_axis=2, concat_axis=0, tiled=...  9.14 us
  transfers between devices with their start and end apart: 3, of which 1 were waited for; matrix products, arithmetic and copies ran while one was open for 29% of the time, Pallas kernels for 0%

commit v1 on v0

--- a/solution.py
+++ b/solution.py
@@ -99,7 +99,8 @@
         scatter_dimension=0,
         tiled=True,
     ).astype(jnp.float32)
-    gain_total = lax.psum(gain_part, ("dp", "seq"))
+    partial = lax.psum(gain_part, "dp")
+    gain_total = lax.psum(partial, "seq")
     return (summed / replicas, gain_total / replicas)
 
 

time: 316 us -> 354 us (1.12)
  waiting for transfers between devices: 48.1 us -> 93.5 us
  blocking collectives: 91.5 us -> 77.2 us
  local copies, waits for them, and re-layouts: 60.3 us -> 64.8 us
    unnamed x3, waiting for transfers between devices: 48.1 us -> 93.5 us
    psum x1, blocking collectives: 41.3 us -> 22.4 us  [on_device(): partial = lax.psum(gain_part, 'dp')]
    psum x2, blocking collectives: 19.5 us -> 27.4 us  [on_device(): lax.psum((jnp.sum(emb_float * emb_float, axis=1), jnp.sum(grad_in * emb_f...]
  transfers between devices with their start and end apart: 3 -> 3, of which waited for: 1 -> 1; matrix products, arithmetic and copies ran while one was open for 29% -> 27% of each run, Pallas kernels for 0% -> 0%
where the time goes in v1:
time: 354 us; the launch traced here: 352 us
  waiting for transfers between devices  93.5 us (26%)
  other arithmetic  84 us (24%)
  blocking collectives  77.2 us (22%)
  local copies, waits for them, and re-layouts  64.8 us (18%)
  between operations  14.3 us (4%)
  matrix products  12 us (3%)
  starting transfers between devices  6.49 us (2%)
    unnamed x3, waiting for transfers between devices  93.5 us
    unnamed x2, other arithmetic  46.5 us
    unnamed x22, local copies, waits for them, and re-layouts  37.7 us
    all_gather x1, blocking collectives, on_device(): gathered = lax.all_gather(tile_tokens[0], 'seq', axis=0, tiled=True)  27.5 us
    psum x2, blocking collectives, on_device(): lax.psum((jnp.sum(emb_float * emb_float, axis=1), jnp.sum(grad_in * emb_f...  27.4 us
    psum x1, blocking collectives, on_device(): partial = lax.psum(gain_part, 'dp')  22.4 us
    convert_element_type x1, other arithmetic, on_device(): quantize(gradient, own_levels, own_row_draws, own_column_draws)  22.1 us
    all_to_all x3, local copies, waits for them, and re-layouts, on_device(): lax.all_to_all(outgoing[None], 'seq', split_axis=2, concat_axis=0, tiled=...  9.14 us
  transfers between devices with their start and end apart: 3, of which 1 were waited for; matrix products, arithmetic and copies ran while one was open for 27% of the time, Pallas kernels for 0%

profile of v1, /device:TPU:0, one launch (start us, length us, event | category | flops | bytes accessed | tf_op | source)
XLA Modules:
  0.0 352.4 jit_solution(5504778816163240057)
XLA Ops:
  7.2 0.0 copy-start
  7.2 0.0 all-gather.3.cloned.1.call-start
  7.2 0.7 all-gather.3.cloned.1.call-update
  7.9 0.7 and_select_fusion.5
  8.6 0.1 convert_reduce_fusion.1
  8.7 0.6 dynamic_slice.12
  9.3 0.2 reduce-window.9
  9.5 0.6 fusion.34
  10.2 0.7 fusion.33
  10.8 1.4 gather_fusion
  12.3 0.7 fusion.31
  13.0 0.0 copy-start.4
  13.0 3.8 %gather_fusion.1 = bf16[48,8192]{1,0:T(8,128)(2,1)S(1)} fusion(bf16[128,8192]{1,0:T(8,128)(2,1)} %bitcast.75, s32[1024]{0:T(1024)S(1)} %pad_clamp_fusion.1), kind=kCustom, calls=%fused_computation.1 | custom fusion | bytes 1573056 | tf_op jit(solution)/shard_map/jit(_take)/gather | solution.py:66
  16.8 1.3 compare_and_fusion
  18.0 1.0 fusion.21
  19.1 8.9 %copy.22 = bf16[1,48,8192]{1,0,2:T(2,128)(2,1)} copy(bf16[1,48,8192]{2,1,0:T(8,128)(2,1)} %fusion.21) | data formatting | bytes 1572864 | tf_op jit(solution)/shard_map/jit(_where)/select_n | solution.py:66
  28.0 0.5 broadcast.575
  28.5 46.5 %reduce.4 = bf16[8192,48]{1,0:T(8,128)(2,1)} reduce(bf16[8192,1,48]{2,1,0:T(2,128)(2,1)} %bitcast.77, bf16[]{:T(256)} %broadcast.575), dimensions={1}, to_apply=%bitcast.63.reduce_sub_computation | reduce | bytes 1572866
  74.9 5.1 %reshape.423 = bf16[4,2,49152]{2,1,0:T(2,128)(2,1)} reshape(bf16[8192,48]{1,0:T(8,128)(2,1)} %reduce.4) | data formatting | bytes 1572864
  80.0 6.5 %all-to-all-start = ((bf16[4,2,49152]{2,1,0:T(2,128)(2,1)}), bf16[4,2,49152]{2,1,0:T(2,128)(2,1)}, u32[]{:S(2)}, u32[]{:S(2)}) async-start(bf16[4,2,49152]{2,1,0:T(2,128)(2,1)} %reshape.423), calls=%async_computation | async-start | bytes 1572864 | tf_op jit(solution)/shard_map/all_to_all | solution.py:67
  86.5 1.0 scatter_custom_fusion
  87.5 2.5 compare_and_fusion.1
  90.0 0.1 dynamic-slice_compare_fusion
  90.1 0.7 dynamic_slice.14
  90.9 2.1 fusion.10
  93.0 27.5 %all-gather = bf16[1,128,3200]{2,1,0:T(8,128)(2,1)S(1)} all-gather(bf16[1,32,3200]{2,1,0:T(8,128)(2,1)S(1)} %copy-done.4), channel_id=2, replica_groups=mesh['dp'=8,'seq'=4] {'seq'}, dimensions={1}, use_global_device_ids=true | all-gather | bytes 1024000 | tf_op jit(solution)/shard_map/all_gather | solution.py:43
  120.5 2.5 fusion.9
  123.0 5.8 %reshape.424 = bf16[8192,1,48]{2,1,0:T(2,128)(2,1)} reshape(bf16[4,2,49152]{2,1,0:T(2,128)(2,1)} %all-to-all-done) | data formatting | bytes 1572864
  128.8 8.1 %copy.23 = bf16[1,48,8192]{2,1,0:T(8,128)(2,1)S(1)} copy(bf16[1,48,8192]{1,0,2:T(2,128)(2,1)} %bitcast.78) | data formatting | bytes 1572864 | tf_op jit(solution)/shard_map/all_to_all | solution.py:67
  136.9 0.6 all_to_all.12
  137.5 0.4 copy.24
  137.9 0.9 gather_fusion.2
  138.9 0.0 all-gather.3.cloned.1.call-done
  138.9 6.9 %multiply_reduce_fusion.1 = (f32[128]{0:T(128)S(1)}, f32[128,2048]{1,0:T(8,128)S(1)}) fusion(bf16[3200,2048]{1,0:T(8,128)(2,1)} %all-gather.3.cloned.1.call-done, bf16[1,128,3200]{2,1,0:T(8,128)(2,1)S(1)} %all-gather), kind=kOutput, calls=%fused_computation.31 | convolution fusion | flops 1678770048 | bytes 14975488 | tf_op jit(solution)/shard_map/dot_general | solution.py:45
  145.8 11.1 %psum.28 = f32[128]{0:T(128)S(1)} all-reduce(f32[128]{0:T(128)S(1)} %get-tuple-element.24), channel_id=1, replica_groups=mesh['dp'=8,'seq'=4] {'seq'}, use_global_device_ids=true, to_apply=%region_3.4 | all-reduce | flops 128 | bytes 1024 | tf_op jit(solution)/shard_map/psum | solution.py:72
  157.0 0.4 fusion.17
  157.4 22.4 %psum.30 = f32[8192]{0:T(1024)S(1)} all-reduce(f32[8192]{0:T(1024)S(1)} %add_dynamic-update-slice_fusion), channel_id=1, replica_groups=mesh['dp'=8,'seq'=4] {'dp'}, use_global_device_ids=true, to_apply=%region_12.13 | all-reduce | flops 8192 | bytes 65536 | tf_op jit(solution)/shard_map/psum | solution.py:102
  179.8 16.3 %all-reduce = (f32[128]{0:T(128)S(1)}, f32[8192]{0:T(1024)S(1)}) all-reduce(f32[128]{0:T(128)S(1)} %get-tuple-element.13, f32[8192]{0:T(1024)S(1)} %psum.30), channel_id=1, replica_groups=mesh['dp'=8,'seq'=4] {'seq'}, use_global_device_ids=true, to_apply=%region_5.6 | all-reduce | flops 8320 | bytes 66560 | tf_op jit(solution)/shard_map/psum | solution.py:72
  196.1 0.0 copy-start.7
  196.1 5.1 %multiply_reduce_fusion = (f32[3200]{0:T(1024)S(1)}, f32[2048,3200]{1,0:T(8,128)S(1)}) fusion(bf16[1,128,3200]{2,1,0:T(8,128)(2,1)S(1)} %all-gather, f32[128,2048]{1,0:T(8,128)} %copy-done.2, f32[128]{0:T(128)S(1)} %multiply_multiply_fusion, f32[128]{0:T(128)S(1)} %add_rsqrt_fusion.1, f32[2048]{0:T(1024)S(1)} %dynamic_slice.14, ...), kind=kOutput, calls=%fused_computation.12 | convolution fusion | flops 1692922752 | bytes 28628608 | tf_op jit(solution)/shard_map/dot_general | solution.py:93
  201.2 22.1 %fusion.6 = bf16[3200,2048]{0,1:T(8,128)(2,1)} fusion(f32[2048,3200]{1,0:T(8,128)S(1)} %get-tuple-element.27, f32[3200]{0:T(1024)S(1)} %convert_reduce_fusion, f32[2048]{0:T(1024)S(1)} %bitcast.80, f32[3200]{0:T(1024)S(1)} %reduce.2, f32[3200]{0:T(1024)S(1)} %add_sqrt_fusion), kind=kLoop, calls=%fused_computation.13 | loop fusion | flops 117964800 | bytes 39368192 | tf_op jit(solution)/shard_map/convert_element_type | solution.py:97
  223.3 18.3 %copy.26 = bf16[3200,2048]{1,0:T(8,128)(2,1)} copy(bf16[3200,2048]{0,1:T(8,128)(2,1)} %fusion.6) | data formatting | bytes 26214400
  241.7 0.0 reduce-scatter.4.cloned.1.call-update
  241.7 0.6 broadcast_multiply_fusion
  242.3 92.8 %reduce-scatter.4.cloned.1.call-done = bf16[400,2048]{1,0:T(8,128)(2,1)} async-done(((bf16[3200,2048]{1,0:T(8,128)(2,1)}), bf16[400,2048]{1,0:T(8,128)(2,1)}) %reduce-scatter.4.cloned.1.call-update) | async-done | bytes 1638416
  335.1 2.8 copy.27
  337.8 2.5 convert_multiply_fusion.2
  340.4 5.2 %copy.25 = f32[400,2048]{1,0:T(8,128)} copy(f32[400,2048]{0,1:T(8,128)} %convert_multiply_fusion.2) | data formatting | bytes 6553600
  (29 shorter events, 0.2 us)
Async XLA Ops:
  7.2 79.3 %copy-start = (s32[1,128]{1,0:T(1,128)S(1)}, s32[1,128]{1,0:T(1,128)}, u32[]{:S(2)}) copy-start(s32[1,128]{1,0:T(1,128)} %param.14) | copy-start | bytes 1540
  7.2 82.8 %copy-start.5 = (s32[1,1,3200]{2,1,0:T(1,128)S(1)}, s32[1,1,3200]{2,1,0:T(1,128)}, u32[]{:S(2)}) copy-start(s32[1,1,3200]{2,1,0:T(1,128)} %param.15) | copy-start | bytes 38404
  7.2 83.6 %copy-start.6 = (f32[1,1,3200]{2,1,0:T(1,128)S(1)}, f32[1,1,3200]{2,1,0:T(1,128)}, u32[]{:S(2)}) copy-start(f32[1,1,3200]{2,1,0:T(1,128)} %param.16) | copy-start | bytes 38404
  7.2 131.7 %all-gather.3.cloned.1.call-start = ((), (), s32[]{:S(2)}) async-start(), calls=%async_computation.2 | async-start | bytes 14745600 | tf_op jit(solution)/shard_map/all_gather | solution.py:47
  13.0 80.0 %copy-start.4 = (bf16[1,32,3200]{2,1,0:T(8,128)(2,1)S(1)}, bf16[1,32,3200]{2,1,0:T(8,128)(2,1)}, u32[]{:S(2)}) copy-start(bf16[1,32,3200]{2,1,0:T(8,128)(2,1)} %param.9) | copy-start | bytes 614404
  13.0 107.5 %copy-start.1 = (bf16[1,128,8192]{2,1,0:T(8,128)(2,1)S(1)}, bf16[1,128,8192]{2,1,0:T(8,128)(2,1)}, u32[]{:S(2)}) copy-start(bf16[1,128,8192]{2,1,0:T(8,128)(2,1)} %param.12) | copy-start | bytes 6291460
  80.0 42.9 %all-to-all-start = ((bf16[4,2,49152]{2,1,0:T(2,128)(2,1)}), bf16[4,2,49152]{2,1,0:T(2,128)(2,1)}, u32[]{:S(2)}, u32[]{:S(2)}) async-start(bf16[4,2,49152]{2,1,0:T(2,128)(2,1)} %reshape.423), calls=%async_computation | async-start | bytes 1572864 | tf_op jit(solution)/shard_map/all_to_all | solution.py:67
  86.5 248.6 %reduce-scatter.4.cloned.1.call-start = ((), (), s32[]{:S(2)}) async-start(), calls=%async_computation.3 | async-start | bytes 14745600
  138.9 57.2 %copy-start.3 = (bf16[128,2048]{1,0:T(8,128)(2,1)}, bf16[128,2048]{1,0:T(8,128)(2,1)S(1)}, u32[]{:S(2)}) copy-start(bf16[128,2048]{1,0:T(8,128)(2,1)S(1)} %gather_fusion.2) | copy-start | bytes 1572868
  145.8 50.2 %copy-start.2 = (f32[128,2048]{1,0:T(8,128)}, f32[128,2048]{1,0:T(8,128)S(1)}, u32[]{:S(2)}) copy-start(f32[128,2048]{1,0:T(8,128)S(1)} %get-tuple-element.25) | copy-start | bytes 3145732
  196.1 5.2 %copy-start.7 = (f32[1,2048]{1,0:T(1,128)S(1)}, f32[1,2048]{1,0:T(1,128)}, u32[]{:S(2)}) copy-start(f32[1,2048]{1,0:T(1,128)} %param.17) | copy-start | bytes 24580
Sparse Core Ops, SparseCore 0:
  9.9 76.9 all-gather.2
  241.8 93.2 reduce-scatter.3
